TPU v7x, 32 devices: a whole 2x2x4 slice. The times are simulated.
32 devices in a mesh: leaf: 2 (over core), row: 4 (over y, x), col: 4 (over z).
Axes of the slice: x: 2, y: 2, z: 4, core: 2. Of those that a mesh axis runs over, the one named last changes fastest.
Arguments:
- rhs_leaf: bfloat16 [2, 8, 64, 2048], P('leaf', None, None, 'col'), may hold values from -6 to 6
- dinv_leaf: bfloat16 [2, 8, 2048, 2048], P('leaf', None, 'row', 'col'), as said below
- panel_leaf: bfloat16 [2, 8, 1024, 2048], P('leaf', None, 'col', 'row'), may hold values from -0.0625 to 0.0625
- counts: int32 [2, 8], P('leaf'), may hold values from 256 to 2048, as said below
- row_index: int32 [2, 8, 1024], P('leaf'), may hold values from 0 to 4095, as said below
- rhs_root: bfloat16 [64, 4096], P(None, 'col'), may hold values from -6 to 6
- dinv_root: bfloat16 [4096, 4096], P(('leaf', 'row')), as said below
Outputs:
- y_leaf: bfloat16 [2, 8, 64, 2048], P('leaf', None, None, 'row')
- y_root: bfloat16 [64, 4096], P(None, ('leaf', 'row'))
Inputs may be any that keep to these rules, and one draw needn't show every extreme that they name: `counts`: each subtree supernode has at least 256 columns; at least one supernode of every draw has all 2048. `row_index`: within one supernode the 1024 entries are distinct and increasing. `dinv_leaf`: each [2048, 2048] block is lower triangular with a nonzero diagonal. `dinv_root`: lower triangular with a nonzero diagonal.
All inputs are finite; a program needn't handle non-finite values.
Results may differ from a plain program's by a relative error of at most 0.0053.
Values may be sent and summed in bfloat16 or wider, within the bound.
No kernel may reach another device: no remote copies, remote signals or barrier semaphores. Data moves between devices by JAX's collectives and lax.ppermute only.
A program may use at most 64 MiB of HBM per device.

v0:
```python
import jax
import jax.numpy as jnp
from jax import lax
from jax.sharding import PartitionSpec as P


def local(rhs_leaf, dinv_leaf, panel_leaf, counts, row_index, rhs_root, dinv_root):
    width_col = rhs_leaf.shape[3]
    width_row = dinv_leaf.shape[2]
    panel_rows = panel_leaf.shape[2]
    columns = rhs_root.shape[0]
    sep_width = rhs_root.shape[1] * lax.axis_size("col")
    limit = counts[0][:, None, None]
    col_slots = lax.axis_index("col") * width_col + lax.iota(jnp.int32, width_col)
    masked = jnp.where(col_slots[None, None, :] < limit, rhs_leaf[0], jnp.zeros((), jnp.bfloat16))
    partial_value = jnp.einsum(
        "kbj,kij->kbi", masked, dinv_leaf[0], preferred_element_type=jnp.float32
    )
    summed = lax.psum(partial_value, "col")
    row_slots = lax.axis_index("row") * width_row + lax.iota(jnp.int32, width_row)
    live_rows = (row_slots[None, None, :] < limit).astype(jnp.float32)
    solved = (summed * live_rows).astype(jnp.bfloat16)
    update = jnp.einsum("kbi,kri->kbr", solved, panel_leaf[0], preferred_element_type=jnp.float32)
    offset = lax.axis_index("col") * panel_rows
    targets = lax.dynamic_slice_in_dim(row_index[0], offset, panel_rows, 1)
    flat_update = jnp.transpose(update, (1, 0, 2)).reshape(columns, -1)
    accum = jnp.zeros((columns, sep_width), jnp.float32).at[:, targets.reshape(-1)].add(flat_update)
    piece = lax.psum_scatter(accum, "col", scatter_dimension=1, tiled=True)
    share = lax.psum(piece, ("leaf", "row"))
    reduced = (rhs_root.astype(jnp.float32) - share).astype(jnp.bfloat16)
    whole_reduced = lax.all_gather(reduced, "col", axis=1, tiled=True)
    y_root = jnp.dot(whole_reduced, dinv_root.T, preferred_element_type=jnp.float32).astype(
        jnp.bfloat16
    )
    return (solved[None], y_root)


def solution(mesh):
    in_specs = (
        P("leaf", None, None, "col"),
        P("leaf", None, "row", "col"),
        P("leaf", None, "col", "row"),
        P("leaf", None),
        P("leaf", None, None),
        P(None, "col"),
        P(("leaf", "row"), None),
    )
    out_specs = (P("leaf", None, None, "row"), P(None, ("leaf", "row")))
    return jax.shard_map(local, mesh=mesh, in_specs=in_specs, out_specs=out_specs, check_vma=False)
```

profile of v0, /device:TPU:0, one launch (start us, length us, event | category | flops | bytes accessed | tf_op | source)
XLA Modules:
  0.0 218.8 jit_solution(5079778243573968000)
XLA Ops:
  7.2 0.0 copy-start
  7.2 0.0 all-reduce.3.cloned.1.call-start
  7.2 0.9 compare_convert_fusion
  8.1 4.7 %fusion = f32[8,64,512]{2,1,0:T(8,128)} fusion(bf16[1,8,512,512]{3,2,1,0:T(8,128)(2,1)} %param.8, bf16[1,8,64,512]{3,2,1,0:T(8,128)(2,1)} %param.7, pred[8,512]{1,0:T(8,128)(4,1)S(1)} %get-tuple-element.3), kind=kOutput, calls=%fused_computation.1 | convolution fusion | flops 268697600 | bytes 5771264 | tf_op jit(solution)/shard_map/kbj,kij->kbi/dot_general | solution.py:16
  12.8 0.0 all-reduce.3.cloned.1.call-update
  12.8 0.0 reduce-scatter.2.cloned.1.call-start
  12.9 0.7 dynamic-slice_bitcast_fusion
  13.6 54.0 %all-reduce.3.cloned.1.call-done = f32[8,64,512]{2,1,0:T(8,128)} async-done(((f32[8,64,512]{2,1,0:T(8,128)}), f32[8,64,512]{2,1,0:T(8,128)}) %all-reduce.3.cloned.1.call-update) | async-done | bytes 1048592 | tf_op jit(solution)/shard_map/psum | solution.py:19
  67.6 0.0 copy-done
  67.6 2.0 fusion.4
  69.6 0.1 copy.13
  69.7 1.3 copy.12
  71.0 0.0 copy-start.2
  71.0 0.0 copy-start.1
  71.0 13.3 %scatter_custom_fusion = f32[64,4096]{0,1:T(8,128)} fusion(s32[2048]{0:T(1024)S(1)} %bitcast.29, f32[2048,64]{1,0:T(8,128)} %copy.12, f32[]{:T(128)} %constant.7.clone.1), kind=kCustom, calls=%fused_computation.7 | custom fusion | flops 131072 | bytes 1049088 | tf_op jit(solution)/shard_map/scatter-add | solution.py:27
  84.3 0.0 reduce-scatter.2.cloned.1.call-update
  84.3 0.0 all-reduce.5.cloned.1.call-start
  84.4 0.0 copy-done.2
  84.4 0.2 copy.10
  84.6 42.8 %reduce-scatter.2.cloned.1.call-done = f32[64,1024]{0,1:T(8,128)} async-done(((f32[64,4096]{0,1:T(8,128)}), f32[64,1024]{0,1:T(8,128)}) %reduce-scatter.2.cloned.1.call-update) | async-done | bytes 262160 | tf_op jit(solution)/shard_map/reduce_scatter | solution.py:28
  127.4 0.0 all-reduce.5.cloned.1.call-update
  127.4 0.0 copy-done.1
  127.4 0.9 fusion.11
  128.4 56.2 %all-reduce.5.cloned.1.call-done = f32[64,1024]{0,1:T(8,128)} async-done(((f32[64,1024]{0,1:T(8,128)}), f32[64,1024]{0,1:T(8,128)}) %all-reduce.5.cloned.1.call-update) | async-done | bytes 262160 | tf_op jit(solution)/shard_map/psum | solution.py:29
  184.5 1.1 subtract_convert_fusion
  185.6 22.4 %all_gather.3 = bf16[64,4096]{0,1:T(8,128)(2,1)S(1)} all-gather(bf16[64,1024]{0,1:T(8,128)(2,1)S(1)} %subtract_convert_fusion), channel_id=1, replica_groups=mesh['leaf'=2,'row'=4,'col'=4] {'col'}, dimensions={1}, use_global_device_ids=true | all-gather | bytes 655360 | tf_op jit(solution)/shard_map/all_gather | solution.py:31
  208.0 4.2 %convolution_convert_fusion = bf16[64,512]{1,0:T(8,128)(2,1)} fusion(bf16[64,4096]{0,1:T(8,128)(2,1)S(1)} %all_gather.3, bf16[512,4096]{1,0:T(8,128)(2,1)} %param.13), kind=kOutput, calls=%fused_computation.6 | convolution fusion | flops 268468224 | bytes 4784128 | tf_op jit(solution)/shard_map/dot_general | solution.py:32
  (3 shorter events, 0.0 us)
Async XLA Ops:
  7.2 60.5 %copy-start = (bf16[1,8,256,512]{3,2,1,0:T(8,128)(2,1)S(1)}, bf16[1,8,256,512]{3,2,1,0:T(8,128)(2,1)}, u32[]{:S(2)}) copy-start(bf16[1,8,256,512]{3,2,1,0:T(8,128)(2,1)} %param.9) | copy-start | bytes 6291460
  7.2 60.4 %all-reduce.3.cloned.1.call-start = ((), (), s32[]{:S(2)}) async-start(), calls=%async_computation.1 | async-start | bytes 2097152 | tf_op jit(solution)/shard_map/psum | solution.py:19
  12.8 114.6 %reduce-scatter.2.cloned.1.call-start = ((), (), s32[]{:S(2)}) async-start(), calls=%async_computation.2 | async-start | bytes 2621440 | tf_op jit(solution)/shard_map/reduce_scatter | solution.py:28
  71.0 13.4 %copy-start.2 = (bf16[64,1024]{1,0:T(8,128)(2,1)S(1)}, bf16[64,1024]{1,0:T(8,128)(2,1)}, u32[]{:S(2)}) copy-start(bf16[64,1024]{1,0:T(8,128)(2,1)} %param.12) | copy-start | bytes 393220
  71.0 56.5 %copy-start.1 = (f32[8,64,512]{2,1,0:T(8,128)S(1)}, f32[8,64,512]{2,1,0:T(8,128)}, u32[]{:S(2)}) copy-start(f32[8,64,512]{2,1,0:T(8,128)} %all-reduce.3.cloned.1.call-done) | copy-start | bytes 3145732
  84.3 100.2 %all-reduce.5.cloned.1.call-start = ((), (), s32[]{:S(2)}) async-start(), calls=%async_computation.3 | async-start | bytes 1048576 | tf_op jit(solution)/shard_map/psum | solution.py:29
Sparse Core Ops, SparseCore 0:
  13.0 54.6 all-reduce.2
  84.5 42.8 reduce-scatter.1
  130.5 53.9 all-reduce.4
where the time goes:
time: 219 us
  waiting for transfers between devices  153 us (70%)
  blocking collectives  22.4 us (10%)
  other arithmetic  16.2 us (7%)
  between operations  13.8 us (6%)
  matrix products  10.9 us (5%)
  local copies, waits for them, and re-layouts  2.27 us (1%)
    psum x1, waiting for transfers between devices, local(): share = lax.psum(piece, ('leaf', 'row'))  56.2 us
    psum x1, waiting for transfers between devices, local(): summed = lax.psum(partial_value, 'col')  54 us
    reduce_scatter x1, waiting for transfers between devices, local(): piece = lax.psum_scatter(accum, 'col', scatter_dimension=1, tiled=True)  42.8 us
    all_gather x1, blocking collectives, local(): whole_reduced = lax.all_gather(reduced, 'col', axis=1, tiled=True)  22.4 us
    scatter-add x1, other arithmetic, local(): jnp.zeros((columns, sep_width), jnp.float32).at[:, targets.reshape(-1)]  13.3 us
    dot_general x1, matrix products, local(): jnp.einsum('kbj,kij->kbi', masked, dinv_leaf[0], preferred_element_type=j...  4.71 us
  transfers between devices with their start and end apart: 3, of which 3 were waited for; matrix products, arithmetic and copies ran while one was open for 1% of the time, Pallas kernels for 0%

commit v1 on v0

--- a/solution.py
+++ b/solution.py
@@ -16,7 +16,7 @@
     partial_value = jnp.einsum(
         "kbj,kij->kbi", masked, dinv_leaf[0], preferred_element_type=jnp.float32
     )
-    summed = lax.psum(partial_value, "col")
+    summed = jnp.sum(lax.all_gather(partial_value, "col"), axis=0)
     row_slots = lax.axis_index("row") * width_row + lax.iota(jnp.int32, width_row)
     live_rows = (row_slots[None, None, :] < limit).astype(jnp.float32)
     solved = (summed * live_rows).astype(jnp.bfloat16)

time: 219 us -> 251 us (1.15)
  waiting for transfers between devices: 153 us -> 181 us
  other arithmetic: 16.2 us -> 18.9 us
    all_gather x0 -> x1, waiting for transfers between devices: none -> 82.8 us  [local(): summed = jnp.sum(lax.all_gather(partial_value, 'col'), axis=0)]
    psum x1 -> x0, waiting for transfers between devices: 54 us -> none  [local(): summed = lax.psum(partial_value, 'col')]
    reduce_sum x0 -> x1, other arithmetic: none -> 2.79 us  [local(): summed = jnp.sum(lax.all_gather(partial_value, 'col'), axis=0)]
where the time goes in v1:
time: 251 us; the launch traced here: 250 us
  waiting for transfers between devices  181 us (72%)
  blocking collectives  22.4 us (9%)
  other arithmetic  18.9 us (8%)
  between operations  13.8 us (5%)
  matrix products  9.69 us (4%)
  local copies, waits for them, and re-layouts  4.12 us (2%)
    all_gather x1, waiting for transfers between devices, local(): summed = jnp.sum(lax.all_gather(partial_value, 'col'), axis=0)  82.8 us
    psum x1, waiting for transfers between devices, local(): share = lax.psum(piece, ('leaf', 'row'))  56.2 us
    reduce_scatter x1, waiting for transfers between devices, local(): piece = lax.psum_scatter(accum, 'col', scatter_dimension=1, tiled=True)  42 us
    all_gather x1, blocking collectives, local(): whole_reduced = lax.all_gather(reduced, 'col', axis=1, tiled=True)  22.4 us
    scatter-add x1, other arithmetic, local(): jnp.zeros((columns, sep_width), jnp.float32).at[:, targets.reshape(-1)]  13.2 us
  transfers between devices with their start and end apart: 3, of which 3 were waited for; matrix products, arithmetic and copies ran while one was open for 1% of the time, Pallas kernels for 0%

profile of v1, /device:TPU:0, one launch (start us, length us, event | category | flops | bytes accessed | tf_op | source)
XLA Modules:
  0.0 250.1 jit_solution(16833162208570134938)
XLA Ops:
  7.2 0.0 copy-start
  7.2 0.0 all-gather.3.cloned.1.call-start
  7.2 0.9 compare_convert_fusion
  8.1 4.7 %fusion = f32[8,64,512]{2,1,0:T(8,128)} fusion(bf16[1,8,512,512]{3,2,1,0:T(8,128)(2,1)} %param.8, bf16[1,8,64,512]{3,2,1,0:T(8,128)(2,1)} %param.7, pred[8,512]{1,0:T(8,128)(4,1)S(1)} %get-tuple-element.3), kind=kOutput, calls=%fused_computation.1 | convolution fusion | flops 268697600 | bytes 5771264 | tf_op jit(solution)/shard_map/kbj,kij->kbi/dot_general | solution.py:16
  12.8 0.0 all-gather.3.cloned.1.call-update
  12.8 0.0 reduce-scatter.2.cloned.1.call-start
  12.9 0.7 dynamic-slice_bitcast_fusion
  13.6 82.8 %all-gather.3.cloned.1.call-done = f32[32,64,512]{2,1,0:T(8,128)} async-done(((f32[8,64,512]{2,1,0:T(8,128)}), f32[32,64,512]{2,1,0:T(8,128)}) %all-gather.3.cloned.1.call-update) | async-done | bytes 4194320 | tf_op jit(solution)/shard_map/all_gather | solution.py:19
  96.5 2.8 %reduce_sum.11 = f32[8,64,512]{2,1,0:T(8,128)S(1)} reduce(f32[4,8,64,512]{3,2,1,0:T(8,128)} %bitcast.30, f32[]{:T(128)} %constant.5.clone.1), dimensions={0}, to_apply=%region_0.1 | reduce | flops 786432 | bytes 5242884 | tf_op jit(solution)/shard_map/reduce_sum | solution.py:19
  99.2 0.0 copy-done
  99.3 0.7 fusion.4
  100.0 0.9 copy.16
  100.9 2.4 copy.15
  103.2 0.0 copy-start.1
  103.2 13.2 %scatter_custom_fusion = f32[64,4096]{0,1:T(8,128)} fusion(s32[2048]{0:T(1024)S(1)} %bitcast.33, f32[2048,64]{1,0:T(8,128)} %copy.15, f32[]{:T(128)} %constant.5.clone.1), kind=kCustom, calls=%fused_computation.10 | custom fusion | flops 131072 | bytes 1049088 | tf_op jit(solution)/shard_map/scatter-add | solution.py:27
  116.5 0.0 reduce-scatter.2.cloned.1.call-update
  116.5 0.0 all-reduce.2.cloned.1.call-start
  116.6 0.0 copy-done.1
  116.6 0.2 copy.13
  116.7 42.0 %reduce-scatter.2.cloned.1.call-done = f32[64,1024]{0,1:T(8,128)} async-done(((f32[64,4096]{0,1:T(8,128)}), f32[64,1024]{0,1:T(8,128)}) %reduce-scatter.2.cloned.1.call-update) | async-done | bytes 262160 | tf_op jit(solution)/shard_map/reduce_scatter | solution.py:28
  158.8 0.0 all-reduce.2.cloned.1.call-update
  158.8 0.9 fusion.7
  159.7 56.2 %all-reduce.2.cloned.1.call-done = f32[64,1024]{0,1:T(8,128)} async-done(((f32[64,1024]{0,1:T(8,128)}), f32[64,1024]{0,1:T(8,128)}) %all-reduce.2.cloned.1.call-update) | async-done | bytes 262160 | tf_op jit(solution)/shard_map/psum | solution.py:29
  215.9 1.1 subtract_convert_fusion
  217.0 22.4 %all_gather.11 = bf16[64,4096]{0,1:T(8,128)(2,1)S(1)} all-gather(bf16[64,1024]{0,1:T(8,128)(2,1)S(1)} %subtract_convert_fusion), channel_id=1, replica_groups=mesh['leaf'=2,'row'=4,'col'=4] {'col'}, dimensions={1}, use_global_device_ids=true | all-gather | bytes 655360 | tf_op jit(solution)/shard_map/all_gather | solution.py:31
  239.4 4.2 %convolution_convert_fusion = bf16[64,512]{1,0:T(8,128)(2,1)} fusion(bf16[64,4096]{0,1:T(8,128)(2,1)S(1)} %all_gather.11, bf16[512,4096]{1,0:T(8,128)(2,1)} %param.13), kind=kOutput, calls=%fused_computation.6 | convolution fusion | flops 268468224 | bytes 4784128 | tf_op jit(solution)/shard_map/dot_general | solution.py:32
  (3 shorter events, 0.0 us)
Async XLA Ops:
  7.2 92.1 %copy-start = (bf16[1,8,256,512]{3,2,1,0:T(8,128)(2,1)S(1)}, bf16[1,8,256,512]{3,2,1,0:T(8,128)(2,1)}, u32[]{:S(2)}) copy-start(bf16[1,8,256,512]{3,2,1,0:T(8,128)(2,1)} %param.9) | copy-start | bytes 6291460
  7.2 89.3 %all-gather.3.cloned.1.call-start = ((), (), s32[]{:S(2)}) async-start(), calls=%async_computation.3 | async-start | bytes 5242880 | tf_op jit(solution)/shard_map/all_gather | solution.py:19
  12.8 145.9 %reduce-scatter.2.cloned.1.call-start = ((), (), s32[]{:S(2)}) async-start(), calls=%async_computation.1 | async-start | bytes 2621440 | tf_op jit(solution)/shard_map/reduce_scatter | solution.py:28
  103.2 13.3 %copy-start.1 = (bf16[64,1024]{1,0:T(8,128)(2,1)S(1)}, bf16[64,1024]{1,0:T(8,128)(2,1)}, u32[]{:S(2)}) copy-start(bf16[64,1024]{1,0:T(8,128)(2,1)} %param.12) | copy-start | bytes 393220
  116.5 99.4 %all-reduce.2.cloned.1.call-start = ((), (), s32[]{:S(2)}) async-start(), calls=%async_computation.2 | async-start | bytes 1048576 | tf_op jit(solution)/shard_map/psum | solution.py:29
Sparse Core Ops, SparseCore 0:
  13.0 83.4 all-gather.2
  116.6 42.1 reduce-scatter.1
  161.9 53.9 all-reduce.1
